TPU v7x, 32 devices: a whole 2x2x4 slice. The times are simulated.
32 devices in a mesh: dp: 4 (over z), row: 4 (over y, x), col: 2 (over core).
Axes of the slice: x: 2, y: 2, z: 4, core: 2. Of those that a mesh axis runs over, the one named last changes fastest.
Arguments:
- tokens: bfloat16 [2048, 1024], P('dp', ('row', 'col')), may hold values from -7.5 to 7.5
- out_grad: bfloat16 [2048, 1024], P('dp', ('row', 'col')), may hold values from -6 to 6
- doc_ids: int32 [2048], P('dp'), may hold values from 0 to 3, never falling along the last dimension, each value on 1 to 1024 neighbouring positions
- expert_ids: int32 [2048, 8], P('dp'), may hold values from 0 to 31, all different within a row
- gain_attn: bfloat16 [1024], P(('row', 'col')), may hold values from 0.5 to 1.5
- w_query: bfloat16 [1024, 1024], P(None, ('row', 'col')), may hold values from -1.1015625 to 1.1015625
- w_key_value: bfloat16 [1024, 8, 128], P(None, ('row', 'col')), may hold values from -0.1875 to 0.1875
- w_output: bfloat16 [1024, 1024], P(('row', 'col')), may hold values from -6 to 6
- gain_moe: bfloat16 [1024], P(('row', 'col')), may hold values from 0.5 to 1.5
- w_router: bfloat16 [1024, 32], P(('row', 'col')), may hold values from -2.75 to 2.75
- w_expert_in: bfloat16 [32, 1024, 2, 512], P('row', None, None, 'col'), may hold values from -0.1875 to 0.1875
- w_expert_out: bfloat16 [32, 512, 1024], P('row', 'col'), may hold values from -4 to 4
Outputs:
- block_out: bfloat16 [2048, 1024], P('dp', ('row', 'col'))
- in_grad: bfloat16 [2048, 1024], P('dp', ('row', 'col'))
- grad_gain_attn: float32 [1024], P(('row', 'col'))
- grad_query: float32 [1024, 1024], P(None, ('row', 'col'))
- grad_key_value: float32 [1024, 8, 128], P(None, ('row', 'col'))
- grad_output: float32 [1024, 1024], P(('row', 'col'))
- grad_gain_moe: float32 [1024], P(('row', 'col'))
- grad_router: float32 [1024, 32], P(('row', 'col'))
- grad_expert_in: float32 [32, 1024, 2, 512], P('row', None, None, 'col')
- grad_expert_out: float32 [32, 512, 1024], P('row', 'col')
Inputs may be any that keep to these rules, and one draw needn't show every extreme that they name: `doc_ids`: never falling along the token stream; every document has 1 to 1024 tokens and one has exactly 1024. `expert_ids`: each row names 8 different experts; every expert is named by some row.
All inputs are finite; a program needn't handle non-finite values.
Results may differ from a plain program's by a relative error of at most 0.02555.
Values may be sent and summed in bfloat16 or wider, within the bound.
A program may use at most 192 MiB of HBM per device.

v0:
```python
import jax
import jax.numpy as jnp
from jax import lax
from jax.sharding import PartitionSpec as P

LONGEST = 4096


HIGH = lax.Precision.HIGHEST
EPSILON = 1e-05
RESIDUAL_SCALE = 0.22
SCORE_SCALE = 0.015625
ROPE_BASE = 10000.0
MASKED = -1e30


def shifted(block, axis, distance):
    devices = range(lax.axis_size(axis))
    route = [(i - distance, i) for i in devices if i - distance in devices]
    return lax.ppermute(block, axis, route)


def rope_tables(positions, head_width):
    half_width = head_width // 2
    freq_table = ROPE_BASE ** (-(2.0 / head_width) * jnp.arange(half_width, dtype=jnp.float32))
    angles = positions.astype(jnp.float32)[:, None] * freq_table[None, :]
    return (jnp.cos(angles), jnp.sin(angles))


def rotate(values, cosine_table, sine_table):
    half_width = values.shape[-1] // 2
    first_half = values[..., :half_width]
    second_half = values[..., half_width:]
    cosine_cols = cosine_table[:, None, :]
    sine_cols = sine_table[:, None, :]
    return jnp.concatenate(
        [
            first_half * cosine_cols - second_half * sine_cols,
            second_half * cosine_cols + first_half * sine_cols,
        ],
        axis=-1,
    )


def unrotate(values, cosine_table, sine_table):
    half_width = values.shape[-1] // 2
    first_half = values[..., :half_width]
    second_half = values[..., half_width:]
    cosine_cols = cosine_table[:, None, :]
    sine_cols = sine_table[:, None, :]
    return jnp.concatenate(
        [
            first_half * cosine_cols + second_half * sine_cols,
            second_half * cosine_cols - first_half * sine_cols,
        ],
        axis=-1,
    )


def masked_scores(query_low, keys_low, query_position, key_position, query_docs, key_docs, present):
    scores = (
        jnp.einsum("qhgc,khc->hgqk", query_low, keys_low, preferred_element_type=jnp.float32)
        * SCORE_SCALE
    )
    allowed = (
        (query_docs[:, None] == key_docs[None, :])
        & (query_position[:, None] >= key_position[None, :])
        & present
    )
    return jnp.where(allowed, scores, MASKED)


def local(
    tokens,
    out_grad,
    doc_ids,
    expert_ids,
    gain_attn,
    w_query,
    w_key_value,
    w_output,
    gain_moe,
    w_router,
    w_expert_in,
    w_expert_out,
):
    tok_rows, feat_local = tokens.shape
    model_width = w_query.shape[0]
    head_dim = w_key_value.shape[2] // 2
    key_heads = w_key_value.shape[1]
    group_size = w_query.shape[1] // head_dim // key_heads
    experts = w_router.shape[1]
    expert_local = w_expert_in.shape[0]
    longest_doc = min(LONGEST, tok_rows * lax.axis_size("dp") // 2)
    hop_count = longest_doc // tok_rows
    grid_size = lax.axis_size(("row", "col"))
    stretch_index = lax.axis_index("dp")
    offsets = jnp.arange(tok_rows, dtype=jnp.int32)
    positions = stretch_index * tok_rows + offsets
    cosine_table, sine_table = rope_tables(positions, head_dim)
    tokens_full, gain_full = (
        lax.all_gather(tokens, ("row", "col"), axis=1, tiled=True),
        lax.all_gather(gain_attn, ("row", "col"), axis=0, tiled=True),
    )
    tokens_wide = tokens_full.astype(jnp.float32)
    gain_wide_attn = gain_full.astype(jnp.float32)
    scale_attn = lax.rsqrt(jnp.mean(tokens_wide * tokens_wide, axis=1) + EPSILON)
    normed_low = (tokens_wide * scale_attn[:, None] * gain_wide_attn).astype(jnp.bfloat16)
    query = jnp.dot(normed_low, w_query, preferred_element_type=jnp.float32).reshape(
        tok_rows, -1, head_dim
    )
    key_value = jnp.einsum(
        "td,dhc->thc", normed_low, w_key_value, preferred_element_type=jnp.float32
    )
    query_low = (
        rotate(query, cosine_table, sine_table)
        .astype(jnp.bfloat16)
        .reshape(tok_rows, key_heads, group_size, head_dim)
    )
    keys_low = rotate(key_value[..., :head_dim], cosine_table, sine_table).astype(jnp.bfloat16)
    values_low = key_value[..., head_dim:].astype(jnp.bfloat16)
    current = (jnp.concatenate([keys_low, values_low], axis=-1), doc_ids.astype(jnp.bfloat16))
    received = [current]
    for distance in range(1, hop_count + 1):
        current = shifted((current[0], current[1]), "dp", 1)
        received.append(current)
    query_docs = doc_ids.astype(jnp.float32)

    def hop_scores(distance):
        key_pair, key_docs = received[distance]
        key_position = (stretch_index - distance) * tok_rows + offsets
        present = stretch_index - distance >= 0
        return masked_scores(
            query_low,
            key_pair[..., :head_dim],
            positions,
            key_position,
            query_docs,
            key_docs.astype(jnp.float32),
            present,
        )

    score_list = [hop_scores(distance) for distance in range(hop_count + 1)]
    row_max = jnp.max(score_list[0], axis=-1)
    for scores in score_list[1:]:
        row_max = jnp.maximum(row_max, jnp.max(scores, axis=-1))
    row_total = jnp.zeros_like(row_max)
    for scores in score_list:
        row_total = row_total + jnp.sum(jnp.exp(scores - row_max[..., None]), axis=-1)
    mixed = jnp.zeros((tok_rows, key_heads, group_size, head_dim), jnp.float32)
    for distance, scores in enumerate(score_list):
        softmax_low = (jnp.exp(scores - row_max[..., None]) / row_total[..., None]).astype(
            jnp.bfloat16
        )
        mixed = mixed + jnp.einsum(
            "hgqk,khc->qhgc",
            softmax_low,
            received[distance][0][..., head_dim:],
            preferred_element_type=jnp.float32,
        )
    log_total = row_max + jnp.log(row_total)
    mixed_low = mixed.astype(jnp.bfloat16).reshape(tok_rows, -1)
    attn_partial = jnp.dot(mixed_low, w_output, preferred_element_type=jnp.float32)
    attn_branch = lax.psum_scatter(
        attn_partial.astype(jnp.bfloat16), ("row", "col"), scatter_dimension=1, tiled=True
    ).astype(jnp.float32)
    tokens_local = tokens.astype(jnp.float32)
    middle = tokens_local + RESIDUAL_SCALE * attn_branch
    chosen = jnp.sum(
        (expert_ids[:, :, None] == jnp.arange(experts, dtype=jnp.int32)[None, None, :]).astype(
            jnp.float32
        ),
        axis=1,
    )
    gain_moe_local = gain_moe.astype(jnp.float32)
    router_local = w_router.astype(jnp.float32)
    squares, raw_logits = lax.psum(
        (
            jnp.sum(middle * middle, axis=1),
            jnp.dot(middle * gain_moe_local, router_local, precision=HIGH),
        ),
        ("row", "col"),
    )
    scale_moe = lax.rsqrt(squares / model_width + EPSILON)
    normed_moe = middle * scale_moe[:, None] * gain_moe_local
    logits = raw_logits * scale_moe[:, None]
    expert_rows = lax.all_gather(
        normed_moe.astype(jnp.bfloat16), ("row", "col"), axis=1, tiled=True
    )
    exp_terms = jnp.exp(logits - jnp.max(logits, axis=1, keepdims=True)) * chosen
    weights = exp_terms / jnp.sum(exp_terms, axis=1, keepdims=True)
    first_expert = lax.axis_index("row") * expert_local
    weights_local = lax.dynamic_slice_in_dim(weights, first_expert, expert_local, 1)
    gate_up = jnp.einsum(
        "td,edgf->tegf", expert_rows, w_expert_in, preferred_element_type=jnp.float32
    )
    gate_value = gate_up[:, :, 0]
    up_value = gate_up[:, :, 1]
    sigmoid_gate = jax.nn.sigmoid(gate_value)
    silu_gate = gate_value * sigmoid_gate
    ungated = silu_gate * up_value
    active_low = (ungated * weights_local[:, :, None]).astype(jnp.bfloat16)
    moe_partial = jnp.einsum(
        "tef,efd->td", active_low, w_expert_out, preferred_element_type=jnp.float32
    )
    moe_branch = lax.psum_scatter(
        moe_partial.astype(jnp.bfloat16), ("row", "col"), scatter_dimension=1, tiled=True
    ).astype(jnp.float32)
    block_out = (middle + RESIDUAL_SCALE * moe_branch).astype(jnp.bfloat16)
    grad_block = out_grad.astype(jnp.float32)
    moe_grad_full = lax.all_gather(
        (RESIDUAL_SCALE * grad_block).astype(jnp.bfloat16), ("row", "col"), axis=1, tiled=True
    )
    active_grad = jnp.einsum(
        "td,efd->tef", moe_grad_full, w_expert_out, preferred_element_type=jnp.float32
    )
    grad_expert_out = jnp.einsum(
        "tef,td->efd", active_low, moe_grad_full, preferred_element_type=jnp.float32
    )
    weight_grad_local = jnp.sum(active_grad * ungated, axis=2)
    ungated_grad = active_grad * weights_local[:, :, None]
    gate_grad = ungated_grad * up_value * sigmoid_gate * (1.0 + gate_value * (1.0 - sigmoid_gate))
    up_grad = ungated_grad * silu_gate
    gate_up_grad = jnp.stack([gate_grad, up_grad], axis=2).astype(jnp.bfloat16)
    grad_expert_in = jnp.einsum(
        "td,tegf->edgf", expert_rows, gate_up_grad, preferred_element_type=jnp.float32
    )
    normed_grad = lax.psum_scatter(
        jnp.einsum(
            "tegf,edgf->td", gate_up_grad, w_expert_in, preferred_element_type=jnp.float32
        ).astype(jnp.bfloat16),
        ("row", "col"),
        scatter_dimension=1,
        tiled=True,
    ).astype(jnp.float32)
    norm_partial = jnp.sum(normed_grad * gain_moe_local * middle, axis=1)
    weight_grad_part = lax.dynamic_update_slice_in_dim(
        jnp.zeros((tok_rows, experts), jnp.float32), weight_grad_local, first_expert, 1
    )
    weight_grad, norm_dot = (
        lax.psum(weight_grad_part.astype(jnp.bfloat16), ("row", "col")).astype(jnp.float32),
        lax.psum(norm_partial.astype(jnp.bfloat16), ("row", "col")).astype(jnp.float32),
    )
    logit_grad = weights * (weight_grad - jnp.sum(weights * weight_grad, axis=1, keepdims=True))
    normed_grad = normed_grad + jnp.dot(logit_grad, router_local.T, precision=HIGH)
    grad_router = jnp.dot(normed_moe.T, logit_grad, precision=HIGH)
    norm_dot = norm_dot + jnp.sum(logit_grad * logits, axis=1) / scale_moe
    grad_gain_moe = jnp.sum(normed_grad * middle * scale_moe[:, None], axis=0)
    middle_grad = (
        grad_block
        + scale_moe[:, None] * gain_moe_local * normed_grad
        - middle * (scale_moe**3 * norm_dot / model_width)[:, None]
    )
    attn_grad_full = lax.all_gather(
        (RESIDUAL_SCALE * middle_grad).astype(jnp.bfloat16), ("row", "col"), axis=1, tiled=True
    )
    grad_output = jnp.einsum(
        "tc,td->cd", mixed_low, attn_grad_full, preferred_element_type=jnp.float32
    )
    mixed_grad = jnp.einsum(
        "td,cd->tc", attn_grad_full, w_output, preferred_element_type=jnp.float32
    )
    mixed_grad_low = mixed_grad.astype(jnp.bfloat16).reshape(
        tok_rows, key_heads, group_size, head_dim
    )
    row_delta = jnp.zeros((key_heads, group_size, tok_rows), jnp.float32)
    softmax_list = []
    product_list = []
    for distance in range(hop_count + 1):
        key_pair = received[distance][0]
        softmax_full = jnp.exp(hop_scores(distance) - log_total[..., None])
        softmax_grad = jnp.einsum(
            "qhgc,khc->hgqk",
            mixed_grad_low,
            key_pair[..., head_dim:],
            preferred_element_type=jnp.float32,
        )
        row_delta = row_delta + jnp.sum(softmax_full * softmax_grad, axis=-1)
        softmax_list.append(softmax_full)
        product_list.append(softmax_grad)
    query_grad = jnp.zeros((tok_rows, key_heads, group_size, head_dim), jnp.float32)
    pieces = []
    for distance in range(hop_count + 1):
        key_pair = received[distance][0]
        softmax_full = softmax_list[distance]
        softmax_low = softmax_full.astype(jnp.bfloat16)
        scores_grad = (softmax_full * (product_list[distance] - row_delta[..., None])).astype(
            jnp.bfloat16
        )
        query_grad = (
            query_grad
            + jnp.einsum(
                "hgqk,khc->qhgc",
                scores_grad,
                key_pair[..., :head_dim],
                preferred_element_type=jnp.float32,
            )
            * SCORE_SCALE
        )
        keys_grad = (
            jnp.einsum("hgqk,qhgc->khc", scores_grad, query_low, preferred_element_type=jnp.float32)
            * SCORE_SCALE
        )
        values_grad = jnp.einsum(
            "hgqk,qhgc->khc", softmax_low, mixed_grad_low, preferred_element_type=jnp.float32
        )
        pieces.append(jnp.concatenate([keys_grad, values_grad], axis=-1))
    carried = pieces[hop_count]
    for distance in range(hop_count - 1, -1, -1):
        carried = (
            shifted(carried.astype(jnp.bfloat16), "dp", -1).astype(carried.dtype) + pieces[distance]
        )
    keys_back = unrotate(carried[..., :head_dim], cosine_table, sine_table)
    key_value_grad = jnp.concatenate([keys_back, carried[..., head_dim:]], axis=-1).astype(
        jnp.bfloat16
    )
    query_grad_low = (
        unrotate(query_grad.reshape(tok_rows, -1, head_dim), cosine_table, sine_table)
        .astype(jnp.bfloat16)
        .reshape(tok_rows, -1)
    )
    grad_query = jnp.einsum(
        "td,tc->dc", normed_low, query_grad_low, preferred_element_type=jnp.float32
    )
    grad_key_value = jnp.einsum(
        "td,thc->dhc", normed_low, key_value_grad, preferred_element_type=jnp.float32
    )
    normed_part = jnp.einsum(
        "tc,dc->td", query_grad_low, w_query, preferred_element_type=jnp.float32
    )
    normed_part = normed_part + jnp.einsum(
        "thc,dhc->td", key_value_grad, w_key_value, preferred_element_type=jnp.float32
    )
    tokens_gain = tokens_wide * gain_wide_attn
    norm_column = jnp.broadcast_to(
        jnp.sum(normed_part * tokens_gain, axis=1)[:, None], (tok_rows, grid_size)
    )
    attn_normed_grad, attn_dot = (
        lax.psum_scatter(
            normed_part.astype(jnp.bfloat16), ("row", "col"), scatter_dimension=1, tiled=True
        ).astype(jnp.float32),
        lax.psum_scatter(
            norm_column.astype(jnp.bfloat16), ("row", "col"), scatter_dimension=1, tiled=True
        ).astype(jnp.float32),
    )
    attn_dot = attn_dot[:, 0]
    gain_attn_local = gain_attn.astype(jnp.float32)
    grad_gain_attn = jnp.sum(attn_normed_grad * tokens_local * scale_attn[:, None], axis=0)
    in_grad = (
        middle_grad
        + scale_attn[:, None] * gain_attn_local * attn_normed_grad
        - tokens_local * (scale_attn**3 * attn_dot / model_width)[:, None]
    ).astype(jnp.bfloat16)
    summed = (
        lax.psum(grad_gain_attn.astype(jnp.bfloat16), "dp").astype(jnp.float32),
        lax.psum(grad_query.astype(jnp.bfloat16), "dp").astype(jnp.float32),
        lax.psum(grad_key_value.astype(jnp.bfloat16), "dp").astype(jnp.float32),
        lax.psum(grad_output.astype(jnp.bfloat16), "dp").astype(jnp.float32),
        lax.psum(grad_gain_moe.astype(jnp.bfloat16), "dp").astype(jnp.float32),
        lax.psum(grad_router.astype(jnp.bfloat16), "dp").astype(jnp.float32),
        lax.psum(grad_expert_in.astype(jnp.bfloat16), "dp").astype(jnp.float32),
        lax.psum(grad_expert_out.astype(jnp.bfloat16), "dp").astype(jnp.float32),
    )
    return (
        block_out,
        in_grad,
        summed[0],
        summed[1],
        summed[2],
        summed[3],
        summed[4],
        summed[5],
        summed[6],
        summed[7],
    )


def solution(mesh):
    in_specs = (
        P("dp", ("row", "col")),
        P("dp", ("row", "col")),
        P("dp"),
        P("dp", None),
        P(("row", "col")),
        P(None, ("row", "col")),
        P(None, ("row", "col"), None),
        P(("row", "col"), None),
        P(("row", "col")),
        P(("row", "col"), None),
        P("row", None, None, "col"),
        P("row", "col", None),
    )
    out_specs = (
        P("dp", ("row", "col")),
        P("dp", ("row", "col")),
        P(("row", "col")),
        P(None, ("row", "col")),
        P(None, ("row", "col"), None),
        P(("row", "col"), None),
        P(("row", "col")),
        P(("row", "col"), None),
        P("row", None, None, "col"),
        P("row", "col", None),
    )
    return jax.shard_map(local, mesh=mesh, in_specs=in_specs, out_specs=out_specs, check_vma=False)
```

profile of v0, /device:TPU:0, one launch (start us, length us, event | category | flops | bytes accessed | tf_op | source)
XLA Modules:
  0.0 925.2 jit_solution(5435885866958941804)
XLA Ops:
  8.7 4.9 collective-permute-start
  15.0 4.2 collective-permute-start.2
  19.2 8.9 all-gather
  28.1 1.6 and_and_fusion.1
  29.7 6.4 all-gather.6.cloned.1.call-done
  36.1 1.6 fusion.8
  37.7 1.8 convolution_bitcast_fusion
  40.0 3.4 collective-permute-start.1
  44.7 1.9 collective-permute-done.1
  46.5 4.4 collective-permute-start.3
  51.5 1.9 collective-permute-done.3
  58.3 2.3 copy.122
  60.7 37.0 %reduce-scatter.13.cloned.1.call-done = bf16[128,512]{1,0:T(8,128)(2,1)} async-done(((bf16[1024,512]{1,0:T(8,128)(2,1)}), bf16[128,512]{1,0:T(8,128)(2,1)}) %reduce-scatter.13.cloned.1.call-update) | async-done | bytes 131088
  98.9 12.3 %psum.84 = f32[512]{0:T(512)S(1)} all-reduce(f32[512]{0:T(512)S(1)} %multiply_reduce_fusion.2), channel_id=1, replica_groups=mesh['dp'=4,'row'=4,'col'=2] {'row','col'}, use_global_device_ids=true, to_apply=%region_9.10 | all-reduce | flops 512 | bytes 4096 | tf_op jit(solution)/shard_map/psum | solution.py:177
  114.5 51.1 %all-reduce.6.cloned.1.call-done = f32[512,32]{0,1:T(8,128)} async-done(((f32[512,32]{0,1:T(8,128)}), f32[512,32]{0,1:T(8,128)}) %all-reduce.6.cloned.1.call-update) | async-done | bytes 65552 | tf_op jit(solution)/shard_map/psum | solution.py:177
  167.8 23.0 %all-gather.8.cloned.1.call-done = bf16[512,1024]{1,0:T(8,128)(2,1)} async-done(((bf16[512,128]{1,0:T(8,128)(2,1)}), bf16[512,1024]{1,0:T(8,128)(2,1)}) %all-gather.8.cloned.1.call-update) | async-done | bytes 1048592 | tf_op jit(solution)/shard_map/all_gather | solution.py:187
  190.8 11.7 %fusion = f32[512,8,2,256]{0,3,2,1:T(8,128)} fusion(bf16[8,1024,2,256]{3,2,1,0:T(2,128)(2,1)} %param.22, bf16[512,1024]{1,0:T(8,128)(2,1)} %all-gather.8.cloned.1.call-done), kind=kOutput, calls=%fused_computation.1 | convolution fusion | flops 4294967296 | bytes 17825792 | tf_op jit(solution)/shard_map/td,edgf->tegf/dot_general | solution.py:194
  202.4 14.1 %all-gather.10.cloned.1.call-done = bf16[512,1024]{1,0:T(8,128)(2,1)} async-done(((bf16[512,128]{1,0:T(8,128)(2,1)}), bf16[512,1024]{1,0:T(8,128)(2,1)}) %all-gather.10.cloned.1.call-update) | async-done | bytes 1048592 | tf_op jit(solution)/shard_map/all_gather | solution.py:211
  216.6 10.1 %multiply_reduce_fusion = (bf16[512,8]{0,1:T(8,128)(2,1)S(1)}, f32[512,8,256]{0,2,1:T(8,128)}) fusion(f32[512,8,2,256]{0,3,2,1:T(8,128)} %fusion, bf16[8,256,1024]{2,1,0:T(8,128)(2,1)} %param.23, bf16[512,1024]{1,0:T(8,128)(2,1)} %all-gather.10.cloned.1.call-done), kind=kOutput, calls=%fused_computation.8 | convolution fusion | flops 2154819584 | bytes 17833984 | tf_op jit(solution)/shard_map/td,efd->tef/dot_general | solution.py:214
  226.7 23.8 %psum.86 = bf16[512,32]{0,1:T(8,128)(2,1)S(1)} all-reduce(bf16[512,32]{0,1:T(8,128)(2,1)S(1)} %constant_dynamic-update-slice_fusion), channel_id=1, replica_groups=mesh['dp'=4,'row'=4,'col'=2] {'row','col'}, use_global_device_ids=true, to_apply=%region_17.18 | all-reduce | flops 16384 | bytes 65536 | tf_op jit(solution)/shard_map/psum | solution.py:241
  251.2 7.1 fusion.23
  260.3 8.9 bitcast_convert_fusion
  269.2 2.3 copy.126
  272.2 35.4 %reduce-scatter.17.cloned.1.call-done = bf16[128,512]{1,0:T(8,128)(2,1)} async-done(((bf16[1024,512]{1,0:T(8,128)(2,1)}), bf16[128,512]{1,0:T(8,128)(2,1)}) %reduce-scatter.17.cloned.1.call-update) | async-done | bytes 131088
  307.6 1.7 copy.127
  309.3 2.0 multiply_reduce_fusion.1
  311.3 13.0 %psum.87 = bf16[512]{0:T(512)(128)(2,1)} all-reduce(bf16[512]{0:T(512)(128)(2,1)} %get-tuple-element.51), channel_id=1, replica_groups=mesh['dp'=4,'row'=4,'col'=2] {'row','col'}, use_global_device_ids=true, to_apply=%region_20.21 | all-reduce | flops 512 | bytes 2048 | tf_op jit(solution)/shard_map/psum | solution.py:242
  325.0 1.5 multiply_convert_fusion.3
  326.6 6.1 bitcast_convert_fusion.1
  332.7 2.3 copy.124
  335.3 14.9 %all-gather.12.cloned.1.call-done = bf16[512,1024]{1,0:T(8,128)(2,1)} async-done(((bf16[512,128]{1,0:T(8,128)(2,1)}), bf16[512,1024]{1,0:T(8,128)(2,1)}) %all-gather.12.cloned.1.call-update) | async-done | bytes 1048592 | tf_op jit(solution)/shard_map/all_gather | solution.py:254
  350.2 1.7 convolution_convert_fusion.5
  351.9 2.2 fusion.45
  356.7 1.5 fusion.17
  358.2 1.8 fusion.55
  363.7 5.3 collective-permute-done.4
  370.7 5.1 collective-permute-done.5
  378.6 6.4 convolution_convert_fusion
  385.0 6.8 convert_bitcast_fusion
  398.3 12.1 %all-reduce = bf16[512,8]{0,1:T(8,128)(2,1)S(1)} all-reduce(bf16[512,8]{0,1:T(8,128)(2,1)S(1)} %broadcast_in_dim.31), channel_id=6, replica_groups=mesh['dp'=4,'row'=4,'col'=2] {'row','col'}, use_global_device_ids=true, to_apply=%region_27.28.clone | all-reduce | flops 4096 | bytes 16384
  411.1 17.5 %reduce-scatter.19.cloned.1.call-done = bf16[128,512]{1,0:T(8,128)(2,1)} async-done(((bf16[1024,512]{1,0:T(8,128)(2,1)}), bf16[128,512]{1,0:T(8,128)(2,1)}) %reduce-scatter.19.cloned.1.call-update) | async-done | bytes 131088
  430.6 12.2 %all-reduce.1 = (bf16[128]{0:T(256)(128)(2,1)S(1)}, bf16[128]{0:T(256)(128)(2,1)S(1)}, bf16[128,32]{0,1:T(8,128)(2,1)S(1)}) all-reduce(bf16[128]{0:T(256)(128)(2,1)S(1)} %get-tuple-element.85, bf16[128]{0:T(256)(128)(2,1)S(1)} %copy-done.51, ...), channel_id=1, replica_groups=mesh['dp'=4,'row'=4,'col'=2] {'dp'}, use_global_device_ids=true, to_apply=%region_29.30 | all-reduce | flops 4352 | bytes 17408 | tf_op jit(solution)/shard_map/psum | solution.py:355
  444.5 439.7 %all-reduce.8.cloned.1.call-done = (bf16[8,1024,2,256]{1,3,2,0:T(8,128)(2,1)}, bf16[1024,128]{1,0:T(8,128)(2,1)}, bf16[1024,1,128]{2,0,1:T(8,128)(2,1)}, bf16[128,1024]{1,0:T(8,128)(2,1)}, bf16[8,256,1024]{2,1,0:T(8,128)(2,1)}) async-done(((bf16[8,1024,2,256]{1,3,2,0:T(8,128)(2,1)}, bf16[1024,128]{1,0:T(8,128)(2,1)}, bf16[1024,1,128]{2,0,1:T(8,128)(2,1)}, bf16[128,1024]{1,0:T(8,128)(2,1)}, ...) | async-done | bytes 13369360 | tf_op jit(solution)/shard_map/psum | solution.py:361
  884.2 1.8 convert_element_type.307
  886.0 1.8 convert_element_type.310
  887.8 1.8 convert_element_type.312
  889.6 21.9 %copy.104 = f32[8,1024,2,256]{3,2,1,0:T(2,128)} copy(bf16[8,1024,2,256]{1,3,2,0:T(8,128)(2,1)} %get-tuple-element.61) | data formatting | bytes 25165824
  911.5 6.6 convert_element_type.321
  (211 shorter events, 42.2 us)
Async XLA Ops:
  7.2 30.6 %copy-start = (bf16[1024,1,128]{2,0,1:T(8,128)(2,1)S(1)}, bf16[1024,1,128]{2,0,1:T(8,128)(2,1)}, u32[]{:S(2)}) copy-start(bf16[1024,1,128]{2,0,1:T(8,128)(2,1)} %param.18) | copy-start | bytes 786436
  7.2 28.9 %all-gather.6.cloned.1.call-start = ((), (), s32[]{:S(2)}) async-start(), calls=%async_computation.4 | async-start | bytes 1179648 | tf_op jit(solution)/shard_map/all_gather | solution.py:102
  7.9 89.8 %reduce-scatter.13.cloned.1.call-start = ((), (), s32[]{:S(2)}) async-start(), calls=%async_computation.9 | async-start | bytes 1179648
  8.7 6.2 collective-permute-start
  13.7 25.9 %copy-start.48 = (f32[32]{0:T(128)}, f32[32]{0:T(128)S(1)}, u32[]{:S(2)}) copy-start(f32[32]{0:T(128)S(1)} %multiply_power_fusion) | copy-start | bytes 388
  15.0 13.1 %collective-permute-start.2 = (bf16[512]{0:T(512)(128)(2,1)S(1)}, bf16[512]{0:T(512)(128)(2,1)S(1)}, u32[]{:S(2)}, u32[]{:S(2)}) collective-permute-start(bf16[512]{0:T(512)(128)(2,1)S(1)} %collective-permute-done), channel_id=1, source_target_pairs={{0,8},{8,16},{16,24},{1,9},{9,17},{17,25},{2,10},{10,18},{18,26},{... | collective-permute-start | bytes 3080 | tf_op jit(solution)/shard_map/ppermute | solution.py:20
  28.1 15.3 %copy-start.40 = (f32[8,1,128]{2,1,0:T(1,128)}, f32[8,1,128]{2,1,0:T(1,128)S(1)}, u32[]{:S(2)}) copy-start(f32[8,1,128]{2,1,0:T(1,128)S(1)} %convert_element_type.322) | copy-start | bytes 12292
  28.1 15.3 %copy-start.28 = (bf16[1024,128]{1,0:T(8,128)(2,1)S(1)}, bf16[1024,128]{1,0:T(8,128)(2,1)}, u32[]{:S(2)}) copy-start(bf16[1024,128]{1,0:T(8,128)(2,1)} %param.17) | copy-start | bytes 786436
  36.1 7.3 copy-start.7
  37.7 6.3 copy-start.36
  39.5 15.3 %copy-start.18 = (f32[512,1,128]{0,2,1:T(8,128)}, f32[512,1,128]{0,2,1:T(8,128)S(1)}, u32[]{:S(2)}) copy-start(f32[512,1,128]{0,2,1:T(8,128)S(1)} %convolution_bitcast_fusion) | copy-start | bytes 786436
  39.9 4.7 copy-start.22
  39.9 4.7 copy-start.24
  40.0 6.6 collective-permute-start.1
  44.0 6.9 copy-start.30
  46.5 8.9 copy-start.32
  46.5 6.9 collective-permute-start.3
  56.9 41.9 %copy-start.5 = (bf16[512,128]{1,0:T(8,128)(2,1)S(1)}, bf16[512,128]{1,0:T(8,128)(2,1)}, u32[]{:S(2)}) copy-start(bf16[512,128]{1,0:T(8,128)(2,1)} %param.12) | copy-start | bytes 393220
  58.3 52.9 %copy-start.45 = (bf16[128,32]{0,1:T(8,128)(2,1)S(1)}, bf16[128,32]{0,1:T(8,128)(2,1)}, u32[]{:S(2)}) copy-start(bf16[128,32]{0,1:T(8,128)(2,1)} %param.21) | copy-start | bytes 24580
  58.3 54.8 %copy-start.13 = (bf16[512,128]{1,0:T(8,128)(2,1)S(1)}, bf16[512,128]{1,0:T(8,128)(2,1)}, u32[]{:S(2)}) copy-start(bf16[512,128]{1,0:T(8,128)(2,1)} %param.13) | copy-start | bytes 393220
  58.3 56.1 %copy-start.39 = (s32[512,8]{0,1:T(8,128)S(1)}, s32[512,8]{0,1:T(8,128)}, u32[]{:S(2)}) copy-start(s32[512,8]{0,1:T(8,128)} %param.15) | copy-start | bytes 49156
  60.6 104.9 %all-reduce.6.cloned.1.call-start = ((), (), s32[]{:S(2)}) async-start(), calls=%async_computation.6 | async-start | bytes 131072 | tf_op jit(solution)/shard_map/psum | solution.py:177
  60.7 130.1 %copy-start.42 = (f32[128]{0:T(128)}, f32[128]{0:T(128)S(1)}, u32[]{:S(2)}) copy-start(f32[128]{0:T(128)S(1)} %convert_element_type.271) | copy-start | bytes 1540
  111.2 79.5 %copy-start.38 = (f32[512]{0:T(512)}, f32[512]{0:T(512)S(1)}, u32[]{:S(2)}) copy-start(f32[512]{0:T(512)S(1)} %psum.84) | copy-start | bytes 6148
  112.2 78.6 %all-gather.8.cloned.1.call-start = ((), (), s32[]{:S(2)}) async-start(), calls=%async_computation.5 | async-start | bytes 1179648 | tf_op jit(solution)/shard_map/all_gather | solution.py:187
  113.1 103.5 %all-gather.10.cloned.1.call-start = ((), (), s32[]{:S(2)}) async-start(), calls=%async_computation.7 | async-start | bytes 1179648 | tf_op jit(solution)/shard_map/all_gather | solution.py:211
  113.8 193.8 %reduce-scatter.17.cloned.1.call-start = ((), (), s32[]{:S(2)}) async-start(), calls=%async_computation.11 | async-start | bytes 1179648
  202.4 48.1 %copy-start.14 = (f32[512,32]{0,1:T(8,128)S(1)}, f32[512,32]{0,1:T(8,128)}, u32[]{:S(2)}) copy-start(f32[512,32]{0,1:T(8,128)} %all-reduce.6.cloned.1.call-done) | copy-start | bytes 196612
  250.5 21.1 %copy-start.26 = (bf16[512,32]{0,1:T(8,128)(2,1)}, bf16[512,32]{0,1:T(8,128)(2,1)S(1)}, u32[]{:S(2)}) copy-start(bf16[512,32]{0,1:T(8,128)(2,1)S(1)} %psum.86) | copy-start | bytes 98308
  251.2 20.4 %copy-start.20 = (f32[512,32]{0,1:T(8,128)}, f32[512,32]{0,1:T(8,128)S(1)}, u32[]{:S(2)}) copy-start(f32[512,32]{0,1:T(8,128)S(1)} %get-tuple-element.69) | copy-start | bytes 196612
  251.2 20.4 %copy-start.46 = (f32[512]{0:T(512)}, f32[512]{0:T(512)S(1)}, u32[]{:S(2)}) copy-start(f32[512]{0:T(512)S(1)} %get-tuple-element.68) | copy-start | bytes 6148
  269.2 40.1 %copy-start.43 = (f32[128]{0:T(128)S(1)}, f32[128]{0:T(128)}, u32[]{:S(2)}) copy-start(f32[128]{0:T(128)} %copy-done.42) | copy-start | bytes 1540
  271.5 78.7 %all-gather.12.cloned.1.call-start = ((), (), s32[]{:S(2)}) async-start(), calls=%async_computation.8 | async-start | bytes 1179648 | tf_op jit(solution)/shard_map/all_gather | solution.py:254
  326.5 70.7 %reduce-scatter.15.cloned.1.call-start = ((), (), s32[]{:S(2)}) async-start(), calls=%async_computation.10 | async-start | bytes 1179648
  335.0 93.5 %reduce-scatter.19.cloned.1.call-start = ((), (), s32[]{:S(2)}) async-start(), calls=%async_computation.12 | async-start | bytes 1179648
  361.4 7.5 collective-permute-start.4
  363.2 12.7 %copy-start.49 = (f32[32]{0:T(128)S(1)}, f32[32]{0:T(128)}, u32[]{:S(2)}) copy-start(f32[32]{0:T(128)} %copy-done.48) | copy-start | bytes 388
  363.2 13.0 %copy-start.8 = (bf16[512,1024]{1,0:T(8,128)(2,1)S(1)}, bf16[512,1024]{1,0:T(8,128)(2,1)}, u32[]{:S(2)}) copy-start(bf16[512,1024]{1,0:T(8,128)(2,1)} %all-gather.6.cloned.1.call-done) | copy-start | bytes 3145732
  363.2 13.0 %copy-start.41 = (f32[8,1,128]{2,1,0:T(1,128)S(1)}, f32[8,1,128]{2,1,0:T(1,128)}, u32[]{:S(2)}) copy-start(f32[8,1,128]{2,1,0:T(1,128)} %copy-done.40) | copy-start | bytes 12292
  369.0 6.9 collective-permute-start.5
  378.3 6.7 copy-start.52
  378.3 506.0 %all-reduce.8.cloned.1.call-start = ((), (), s32[]{:S(2)}) async-start(), calls=%async_computation.13 | async-start | bytes 26738688 | tf_op jit(solution)/shard_map/psum | solution.py:361
  378.6 6.4 copy-start.10
  378.6 6.4 copy-start.12
  385.0 6.8 copy-start.6
  385.0 6.8 copy-start.17
  385.0 7.8 copy-start.37
  395.6 35.0 %copy-start.51 = (bf16[128]{0:T(256)(128)(2,1)S(1)}, bf16[128]{0:T(256)(128)(2,1)}, u32[]{:S(2)}) copy-start(bf16[128]{0:T(256)(128)(2,1)} %get-tuple-element.50) | copy-start | bytes 772
  (23 other events, 45.8 us)
Sparse Core Ops, SparseCore 0:
  9.9 26.1 all-gather.5
  60.8 36.9 reduce-scatter.12
  112.3 53.1 all-reduce.5
  167.9 22.8 all-gather.7
  193.1 23.4 all-gather.9
  271.6 35.9 reduce-scatter.16
  326.7 23.4 all-gather.11
  353.3 36.0 reduce-scatter.14
  392.6 35.9 reduce-scatter.18
  432.7 451.4 all-reduce.7
where the time goes:
time: 933 us; the launch traced here: 925 us
  waiting for transfers between devices  655 us (70%)
  blocking collectives  82.4 us (9%)
  matrix products  74.5 us (8%)
  local copies, waits for them, and re-layouts  39.5 us (4%)
  other arithmetic  37.6 us (4%)
  starting transfers between devices  20.9 us (2%)
  between operations  15.4 us (2%)
    psum x1, waiting for transfers between devices, local(): lax.psum(grad_expert_in.astype(jnp.bfloat16), 'dp').astype(jnp.float32)  440 us
    unnamed x14, waiting for transfers between devices  90.8 us
    psum x1, waiting for transfers between devices, local(): lax.psum((jnp.sum(middle * middle, axis=1), jnp.dot(middle * gain_moe_loc...  51.1 us
    unnamed x120, local copies, waits for them, and re-layouts  39.4 us
    psum x1, blocking collectives, local(): lax.psum(weight_grad_part.astype(jnp.bfloat16), ('row', 'col'))  23.8 us
    all_gather x1, waiting for transfers between devices, local(): lax.all_gather(normed_moe.astype(jnp.bfloat16), ('row', 'col'), axis=1, t...  23 us
    ppermute x6, starting transfers between devices, shifted(): return lax.ppermute(block, axis, route)  19.5 us
  transfers between devices with their start and end apart: 16, of which 14 were waited for; matrix products, arithmetic and copies ran while one was open for 7% of the time, Pallas kernels for 0%

commit v1 on v0

v1 whole, which is shorter than its diff:
```python
import functools

import jax
import jax.numpy as jnp
from jax import lax
from jax.experimental import pallas as pl
from jax.experimental.pallas import tpu as pltpu
from jax.sharding import PartitionSpec as P

LONGEST = 4096
HIGH = lax.Precision.HIGHEST
EPSILON = 1e-05
RESIDUAL_SCALE = 0.22
SCORE_SCALE = 0.015625
ROPE_BASE = 10000.0
MASKED = -1e30
MESH = pl.DeviceIdType.MESH
GROUP = ("row", "col")
EVERY = ("dp", "row", "col")
LANES = 128
HBM = pl.BlockSpec(memory_space=pl.ANY)


def exchange_body(sizes, kinds, *refs):
    rows, cols, depth = sizes
    count = len(kinds)
    sources, targets = refs[:count], refs[count : 2 * count]
    send_sem, recv_sem, local_sem = refs[2 * count :]
    row, col, layer = lax.axis_index("row"), lax.axis_index("col"), lax.axis_index("dp")
    group = rows * cols
    me = row * cols + col
    barrier = pltpu.get_barrier_semaphore()
    partners = []
    if any(kind[0] == "swap" for kind in kinds):
        for k in range(1, group):
            other = lax.rem(me + k, group)
            partners.append({"row": other // cols, "col": lax.rem(other, cols)})
    elif any(kind[0] == "gather" for kind in kinds):
        for k in range(1, rows):
            partners.append({"row": lax.rem(row + k, rows)})
        for k in range(1, cols):
            partners.append({"col": lax.rem(col + k, cols)})
    shifts = set()
    for kind in kinds:
        if kind[0] == "shift":
            for d in kind[1]:
                shifts |= {d % depth, -d % depth}
    for k in sorted(shifts - {0}):
        partners.append({"dp": lax.rem(layer + k, depth)})
    for partner in partners:
        pl.semaphore_signal(barrier, inc=1, device_id=partner, device_id_type=MESH)
    pl.semaphore_wait(barrier, len(partners))

    slot = 0
    remote, local, relays = [], [], []

    def send(source, target, device):
        nonlocal slot
        copy = pltpu.make_async_remote_copy(
            src_ref=source,
            dst_ref=target,
            send_sem=send_sem.at[slot],
            recv_sem=recv_sem.at[slot],
            device_id=device,
            device_id_type=MESH,
        )
        slot += 1
        copy.start()
        return copy

    for index, (kind, source, target) in enumerate(zip(kinds, sources, targets)):
        if kind[0] == "gather":
            for k in range(1, rows):
                copy = send(source, target.at[me], {"row": lax.rem(row + k, rows)})
                origin = lax.rem(row + rows - k, rows) * cols + col
                relays.append((copy, target, origin))
            for k in range(1, cols):
                remote.append(send(source, target.at[me], {"col": lax.rem(col + k, cols)}))
            local.append(pltpu.make_async_copy(source, target.at[me], local_sem.at[index]))
        elif kind[0] == "swap":
            for k in range(1, group):
                other = lax.rem(me + k, group)
                device = {"row": other // cols, "col": lax.rem(other, cols)}
                remote.append(send(source.at[other], target.at[me], device))
            local.append(
                pltpu.make_async_copy(source.at[me], target.at[me], local_sem.at[index])
            )
        else:
            for at, d in enumerate(kind[1]):
                piece = source.at[at] if kind[2] else source
                device = {"dp": lax.rem(layer + d % depth, depth)}
                remote.append(send(piece, target.at[at], device))
    for copy in local:
        copy.start()
    for copy, target, origin in relays:
        copy.wait_recv()
        for k in range(1, cols):
            device = {"col": lax.rem(col + k, cols)}
            remote.append(send(target.at[origin], target.at[origin], device))
    for copy, _, _ in relays:
        copy.wait_send()
    for copy in remote:
        copy.wait()
    for copy in local:
        copy.wait()


def exchange(sizes, name, number, *items):
    rows, cols, depth = sizes
    group = rows * cols
    kinds, arrays, shapes, copies = [], [], [], 0
    for item in items:
        array = item[1]
        arrays.append(array)
        if item[0] == "gather":
            kinds.append(("gather",))
            shapes.append(jax.ShapeDtypeStruct((group,) + array.shape, array.dtype))
            copies += (rows - 1) * cols + cols - 1
        elif item[0] == "swap":
            kinds.append(("swap",))
            shapes.append(jax.ShapeDtypeStruct(array.shape, array.dtype))
            copies += group - 1
        else:
            distances, split = item[2], item[3]
            kinds.append(("shift", tuple(distances), split))
            block = array.shape[1:] if split else array.shape
            shapes.append(jax.ShapeDtypeStruct((len(distances),) + block, array.dtype))
            copies += len(distances)
    return pl.pallas_call(
        functools.partial(exchange_body, sizes, tuple(kinds)),
        out_shape=tuple(shapes),
        in_specs=[HBM] * len(arrays),
        out_specs=(HBM,) * len(arrays),
        scratch_shapes=[
            pltpu.SemaphoreType.DMA((copies,)),
            pltpu.SemaphoreType.DMA((copies,)),
            pltpu.SemaphoreType.DMA((len(arrays),)),
        ],
        compiler_params=pltpu.CompilerParams(collective_id=number, has_side_effects=True),
        name=name,
    )(*arrays)


def rope_tables(positions, head_width):
    half_width = head_width // 2
    freq_table = ROPE_BASE ** (-(2.0 / head_width) * jnp.arange(half_width, dtype=jnp.float32))
    angles = positions.astype(jnp.float32)[:, None] * freq_table[None, :]
    return (jnp.cos(angles), jnp.sin(angles))


def rotate(values, cosine_table, sine_table):
    half_width = values.shape[-1] // 2
    first_half = values[..., :half_width]
    second_half = values[..., half_width:]
    cosine_cols = cosine_table[:, None, :]
    sine_cols = sine_table[:, None, :]
    return jnp.concatenate(
        [
            first_half * cosine_cols - second_half * sine_cols,
            second_half * cosine_cols + first_half * sine_cols,
        ],
        axis=-1,
    )


def masked_scores(query_low, keys_low, query_position, key_position, query_docs, key_docs, present):
    scores = (
        jnp.einsum("qhgc,khc->hgqk", query_low, keys_low, preferred_element_type=jnp.float32)
        * SCORE_SCALE
    )
    allowed = (
        (query_docs[:, None] == key_docs[None, :])
        & (query_position[:, None] >= key_position[None, :])
        & present
    )
    return jnp.where(allowed, scores, MASKED)


def dot(a, b, left=1, right=0):
    return lax.dot_general(
        a, b, (((left,), (right,)), ((), ())), preferred_element_type=jnp.float32
    )


def column_of(block, column):
    lanes = lax.broadcasted_iota(jnp.int32, block.shape, 1)
    return jnp.sum(jnp.where(lanes == column, block, 0.0), axis=1, keepdims=True)


def expert_terms(rows, grads, weight, w_in, w_out):
    hidden = w_out.shape[0]
    gate_up = dot(rows, w_in)
    gate, up = gate_up[:, :hidden], gate_up[:, hidden:]
    active_grad = dot(grads, w_out, 1, 1)
    sigmoid = jax.nn.sigmoid(gate)
    silu = gate * sigmoid
    ungated = silu * up
    active = (ungated * weight).astype(jnp.bfloat16)
    scaled = active_grad * weight
    gate_grad = (scaled * up * sigmoid * (1.0 + gate * (1.0 - sigmoid))).astype(jnp.bfloat16)
    up_grad = (scaled * silu).astype(jnp.bfloat16)
    return active, jnp.concatenate([gate_grad, up_grad], axis=1), active_grad * ungated


def local_experts_body(first_of, rows_ref, grads_ref, weight_ref, in_ref, out_ref, moe_ref, back_ref, share_ref, moe_acc, back_acc, share_acc):
    expert = pl.program_id(0)

    @pl.when(expert == 0)
    def _():
        moe_acc[...] = jnp.zeros_like(moe_acc)
        back_acc[...] = jnp.zeros_like(back_acc)
        share_acc[...] = jnp.zeros_like(share_acc)

    w_in, w_out = in_ref[0], out_ref[0]
    weight = column_of(weight_ref[...], first_of(pl.num_programs(0)) + expert)
    active, gate_up_grad, shares = expert_terms(rows_ref[...], grads_ref[...], weight, w_in, w_out)
    moe_acc[...] += dot(active, w_out)
    back_acc[...] += dot(gate_up_grad, w_in, 1, 1)
    lanes = lax.broadcasted_iota(jnp.int32, share_acc.shape, 1)
    share = jnp.sum(shares, axis=1, keepdims=True)
    share_acc[...] = jnp.where(lanes == expert, share, share_acc[...])

    @pl.when(expert == pl.num_programs(0) - 1)
    def _():
        moe_ref[...] = moe_acc[...].astype(jnp.bfloat16)
        back_ref[...] = back_acc[...].astype(jnp.bfloat16)
        share_ref[...] = share_acc[...].astype(jnp.bfloat16)


def first_expert(count):
    return lax.axis_index("row") * count


def local_experts(rows, grads, weight, w_in, w_out):
    tokens, width = rows.shape
    experts, hidden = w_out.shape[0], w_out.shape[1]
    whole = lambda a: pl.BlockSpec(a.shape, lambda e: (0, 0))
    outs = [(tokens, width), (tokens, width), (tokens, LANES)]
    return pl.pallas_call(
        functools.partial(local_experts_body, first_expert),
        grid=(experts,),
        in_specs=[
            whole(rows),
            whole(grads),
            whole(weight),
            pl.BlockSpec((1, width, 2 * hidden), lambda e: (e, 0, 0)),
            pl.BlockSpec((1, hidden, width), lambda e: (e, 0, 0)),
        ],
        out_specs=tuple(pl.BlockSpec(s, lambda e: (0, 0)) for s in outs),
        out_shape=tuple(jax.ShapeDtypeStruct(s, jnp.bfloat16) for s in outs),
        scratch_shapes=[pltpu.VMEM(s, jnp.float32) for s in outs],
        name="local_experts",
    )(rows, grads, weight, w_in, w_out)


def expert_grads_body(first_of, rows_ref, grads_ref, weight_ref, in_ref, out_ref, gin_ref, gout_ref, in_acc, out_acc):
    expert, tile = pl.program_id(0), pl.program_id(1)
    hidden = out_ref.shape[1]

    @pl.when(tile == 0)
    def _():
        in_acc[...] = jnp.zeros_like(in_acc)
        out_acc[...] = jnp.zeros_like(out_acc)

    rows, grads = rows_ref[...], grads_ref[...]
    weights = weight_ref[...].astype(jnp.float32)
    column = first_of(pl.num_programs(0)) + expert
    weight = column_of(weights, column) + column_of(weights, column + LANES // 2)
    active, gate_up_grad, _ = expert_terms(rows, grads, weight, in_ref[0], out_ref[0])
    in_acc[...] += dot(rows, gate_up_grad, 0, 0)
    out_acc[...] += dot(active, grads, 0, 0)

    @pl.when(tile == pl.num_programs(1) - 1)
    def _():
        gout_ref[0] = out_acc[...]
        width = in_acc.shape[0]
        parts = hidden // LANES
        for part in range(parts):
            for half in range(2):
                at = half * hidden + part * LANES
                gin_ref[0, pl.ds(part * 2 + half, width, stride=2 * parts), :] = in_acc[
                    :, at : at + LANES
                ]


def expert_grads(rows, grads, weight, w_in, w_out):
    tokens, width = rows.shape
    experts, hidden = w_out.shape[0], w_out.shape[1]
    tile = 512
    parts = hidden // LANES
    gin, gout = pl.pallas_call(
        functools.partial(expert_grads_body, first_expert),
        grid=(experts, tokens // tile),
        in_specs=[
            pl.BlockSpec((tile, width), lambda e, t: (t, 0)),
            pl.BlockSpec((tile, width), lambda e, t: (t, 0)),
            pl.BlockSpec((tile, LANES), lambda e, t: (t, 0)),
            pl.BlockSpec((1, width, 2 * hidden), lambda e, t: (e, 0, 0)),
            pl.BlockSpec((1, hidden, width), lambda e, t: (e, 0, 0)),
        ],
        out_specs=(
            pl.BlockSpec((1, width * 2 * parts, LANES), lambda e, t: (e, 0, 0)),
            pl.BlockSpec((1, hidden, width), lambda e, t: (e, 0, 0)),
        ),
        out_shape=(
            jax.ShapeDtypeStruct((experts, width * 2 * parts, LANES), jnp.float32),
            jax.ShapeDtypeStruct((experts, hidden, width), jnp.float32),
        ),
        scratch_shapes=[
            pltpu.VMEM((width, 2 * hidden), jnp.float32),
            pltpu.VMEM((hidden, width), jnp.float32),
        ],
        name="expert_grads",
    )(rows, grads, weight, w_in, w_out)
    gin = gin.reshape(experts, width, parts, 2, LANES).transpose(0, 1, 3, 2, 4)
    return gin.reshape(experts, width, 2, hidden), gout


def local(
    sizes,
    tokens,
    out_grad,
    doc_ids,
    expert_ids,
    gain_attn,
    w_query,
    w_key_value,
    w_output,
    gain_moe,
    w_router,
    w_expert_in,
    w_expert_out,
):
    rows, cols, depth = sizes
    group = rows * cols
    tok_rows, feat_local = tokens.shape
    width = w_query.shape[0]
    head_dim = w_key_value.shape[2] // 2
    key_heads = w_key_value.shape[1]
    group_size = w_query.shape[1] // head_dim // key_heads
    experts = w_router.shape[1]
    expert_local, hidden = w_expert_out.shape[0], w_expert_out.shape[1]
    longest_doc = min(LONGEST, tok_rows * depth // 2)
    hop_count = longest_doc // tok_rows
    own = tok_rows // group
    layer = lax.axis_index("dp")
    me = lax.axis_index("row") * cols + lax.axis_index("col")
    offsets = jnp.arange(tok_rows, dtype=jnp.int32)
    positions = layer * tok_rows + offsets
    cosine_table, sine_table = rope_tables(positions, head_dim)

    def wide(blocks):
        return jnp.moveaxis(blocks, 0, 1).reshape(blocks.shape[1], -1)

    def narrow(array):
        return jnp.moveaxis(array.reshape(array.shape[0], group, -1), 1, 0)

    def gathered(array, axes, axis):
        return lax.all_gather(array, axes, axis=axis, tiled=True)

    docs_all = gathered(doc_ids, "dp", 0)
    gains = gathered(jnp.stack([gain_attn, gain_moe]), GROUP, 1).astype(jnp.float32)
    router_full = gathered(w_router, GROUP, 0).astype(jnp.float32)
    output_full = gathered(w_output, GROUP, 0)
    scaled_grad = (RESIDUAL_SCALE * out_grad.astype(jnp.float32)).astype(jnp.bfloat16)

    tokens_blocks, grad_blocks = exchange(
        sizes, "gather_tokens", 0, ("gather", tokens), ("gather", out_grad)
    )
    tokens_full = wide(tokens_blocks)
    tokens_wide = tokens_full.astype(jnp.float32)
    grad_full = wide(grad_blocks)
    moe_grad_full = (RESIDUAL_SCALE * grad_full.astype(jnp.float32)).astype(jnp.bfloat16)
    moe_grad_own = lax.dynamic_slice_in_dim(moe_grad_full, me * own, own, 0)
    moe_grad_all = gathered(moe_grad_own, EVERY, 0)
    query_full = gathered(w_query, GROUP, 1)
    key_value_full = gathered(w_key_value, GROUP, 1)

    scale_attn = lax.rsqrt(jnp.mean(tokens_wide * tokens_wide, axis=1) + EPSILON)
    normed_low = (tokens_wide * scale_attn[:, None] * gains[0]).astype(jnp.bfloat16)
    query = dot(normed_low, w_query).reshape(tok_rows, -1, head_dim)
    key_value = jnp.einsum(
        "td,dhc->thc", normed_low, w_key_value, preferred_element_type=jnp.float32
    )
    query_low = (
        rotate(query, cosine_table, sine_table)
        .astype(jnp.bfloat16)
        .reshape(tok_rows, key_heads, group_size, head_dim)
    )
    keys_low = rotate(key_value[..., :head_dim], cosine_table, sine_table).astype(jnp.bfloat16)
    values_low = key_value[..., head_dim:].astype(jnp.bfloat16)
    pair = jnp.concatenate([keys_low, values_low], axis=-1).reshape(tok_rows, -1)
    hops = list(range(1, hop_count + 1))
    (received_pairs,) = exchange(sizes, "shift_pairs", 1, ("shift", pair, hops, False))
    pairs = [pair] + [received_pairs[i] for i in range(hop_count)]
    received = [p.reshape(tok_rows, key_heads, 2 * head_dim) for p in pairs]

    def hop_scores(distance):
        origin = lax.rem(layer + depth - distance, depth)
        key_docs = lax.dynamic_slice_in_dim(docs_all, origin * tok_rows, tok_rows, 0)
        return masked_scores(
            query_low,
            received[distance][..., :head_dim],
            positions,
            (layer - distance) * tok_rows + offsets,
            doc_ids,
            key_docs,
            layer - distance >= 0,
        )

    score_list = [hop_scores(distance) for distance in range(hop_count + 1)]
    row_max = jnp.max(score_list[0], axis=-1)
    for scores in score_list[1:]:
        row_max = jnp.maximum(row_max, jnp.max(scores, axis=-1))
    row_total = jnp.zeros_like(row_max)
    for scores in score_list:
        row_total = row_total + jnp.sum(jnp.exp(scores - row_max[..., None]), axis=-1)
    mixed = jnp.zeros((tok_rows, key_heads, group_size, head_dim), jnp.float32)
    for distance, scores in enumerate(score_list):
        softmax_low = (jnp.exp(scores - row_max[..., None]) / row_total[..., None]).astype(
            jnp.bfloat16
        )
        mixed = mixed + jnp.einsum(
            "hgqk,khc->qhgc",
            softmax_low,
            received[distance][..., head_dim:],
            preferred_element_type=jnp.float32,
        )
    log_total = row_max + jnp.log(row_total)
    mixed_low = mixed.astype(jnp.bfloat16).reshape(tok_rows, -1)
    (mixed_blocks,) = exchange(
        sizes, "swap_mixed", 2, ("swap", mixed_low.reshape(group, own, -1))
    )

    mixed_own = wide(mixed_blocks)
    tokens_own = lax.dynamic_slice_in_dim(tokens_full, me * own, own, 0).astype(jnp.float32)
    middle = tokens_own + RESIDUAL_SCALE * dot(mixed_own, output_full)
    scale_moe = lax.rsqrt(jnp.mean(middle * middle, axis=1, keepdims=True) + EPSILON)
    normed_moe = middle * scale_moe * gains[1]
    logits = jnp.dot(normed_moe, router_full, precision=HIGH)
    ids_own = lax.dynamic_slice_in_dim(expert_ids, me * own, own, 0)
    chosen = jnp.sum(
        (ids_own[:, :, None] == jnp.arange(experts, dtype=jnp.int32)[None, None, :]).astype(
            jnp.float32
        ),
        axis=1,
    )
    exp_terms = jnp.exp(logits - jnp.max(logits, axis=1, keepdims=True)) * chosen
    weights = exp_terms / jnp.sum(exp_terms, axis=1, keepdims=True)
    weights_high = weights.astype(jnp.bfloat16)
    weights_low = (weights - weights_high.astype(jnp.float32)).astype(jnp.bfloat16)
    blank = jnp.zeros((own, LANES // 2 - experts), jnp.bfloat16)
    weights_pair = jnp.concatenate([weights_high, blank, weights_low, blank], axis=1)
    normed_own = normed_moe.astype(jnp.bfloat16)
    rows_blocks, weight_blocks = exchange(
        sizes, "gather_rows", 3, ("gather", normed_own), ("gather", weights_pair)
    )
    rows_all = gathered(normed_own, EVERY, 0)
    weights_all = gathered(weights_pair, EVERY, 0)
    rows_full = rows_blocks.reshape(tok_rows, width)
    weights_full = weight_blocks.reshape(tok_rows, LANES).astype(jnp.float32)
    half = LANES // 2
    weights_wide = weights_full + jnp.roll(weights_full, -half, axis=1)

    in_flat = w_expert_in.reshape(expert_local, width, 2 * hidden)
    moe_partial, back_partial, share_partial = local_experts(
        rows_full, moe_grad_full, weights_wide, in_flat, w_expert_out
    )
    moe_own = lax.psum_scatter(moe_partial, GROUP, scatter_dimension=0, tiled=True)
    back_blocks, share_blocks = exchange(
        sizes,
        "swap_back",
        4,
        ("swap", back_partial.reshape(group, own, width)),
        ("swap", share_partial.reshape(group, own, LANES)),
    )
    normed_grad = jnp.sum(back_blocks.astype(jnp.float32), axis=0)
    shares = jnp.sum(share_blocks.astype(jnp.float32).reshape(rows, cols, own, LANES), axis=1)
    weight_grad = jnp.moveaxis(shares[:, :, :expert_local], 0, 1).reshape(own, experts)
    logit_grad = weights * (weight_grad - jnp.sum(weights * weight_grad, axis=1, keepdims=True))
    normed_grad = normed_grad + jnp.dot(logit_grad, router_full.T, precision=HIGH)
    gain_moe_part = jnp.sum(normed_grad * middle * scale_moe, axis=0)
    grad_own = lax.dynamic_slice_in_dim(grad_full, me * own, own, 0).astype(jnp.float32)
    norm_dot = jnp.sum(normed_grad * gains[1] * middle, axis=1, keepdims=True)
    middle_grad = (
        grad_own + scale_moe * gains[1] * normed_grad - middle * (scale_moe**3 * norm_dot / width)
    )
    attn_grad = (RESIDUAL_SCALE * middle_grad).astype(jnp.bfloat16)
    mixed_grad_own = dot(attn_grad, output_full, 1, 1).astype(jnp.bfloat16)
    (mixed_grad_blocks,) = exchange(
        sizes, "swap_mixed_grad", 5, ("swap", narrow(mixed_grad_own))
    )
    logit_grad_all = gathered(logit_grad.astype(jnp.bfloat16), EVERY, 0)
    attn_grad_full = gathered(attn_grad, GROUP, 0)
    grad_output = dot(mixed_low, attn_grad_full, 0, 0)
    grad_output = lax.psum(grad_output.astype(jnp.bfloat16), "dp").astype(jnp.float32)

    mixed_grad_low = mixed_grad_blocks.reshape(tok_rows, key_heads, group_size, head_dim)
    row_delta = jnp.zeros((key_heads, group_size, tok_rows), jnp.float32)
    softmax_list = []
    product_list = []
    for distance in range(hop_count + 1):
        softmax_full = jnp.exp(score_list[distance] - log_total[..., None])
        softmax_grad = jnp.einsum(
            "qhgc,khc->hgqk",
            mixed_grad_low,
            received[distance][..., head_dim:],
            preferred_element_type=jnp.float32,
        )
        row_delta = row_delta + jnp.sum(softmax_full * softmax_grad, axis=-1)
        softmax_list.append(softmax_full)
        product_list.append(softmax_grad)
    query_grad = jnp.zeros((tok_rows, key_heads, group_size, head_dim), jnp.float32)
    pieces = []
    for distance in range(hop_count + 1):
        softmax_full = softmax_list[distance]
        scores_grad = (softmax_full * (product_list[distance] - row_delta[..., None])).astype(
            jnp.bfloat16
        )
        query_grad = (
            query_grad
            + jnp.einsum(
                "hgqk,khc->qhgc",
                scores_grad,
                received[distance][..., :head_dim],
                preferred_element_type=jnp.float32,
            )
            * SCORE_SCALE
        )
        keys_grad = (
            jnp.einsum("hgqk,qhgc->khc", scores_grad, query_low, preferred_element_type=jnp.float32)
            * SCORE_SCALE
        )
        values_grad = jnp.einsum(
            "hgqk,qhgc->khc",
            softmax_full.astype(jnp.bfloat16),
            mixed_grad_low,
            preferred_element_type=jnp.float32,
        )
        pieces.append(jnp.concatenate([keys_grad, values_grad], axis=-1).reshape(tok_rows, -1))
    sent = jnp.stack(pieces[1:]).astype(jnp.bfloat16)
    (returned,) = exchange(
        sizes, "shift_grads", 6, ("shift", sent, [-d for d in hops], True)
    )
    carried = pieces[0]
    for distance in hops:
        carried = carried + jnp.where(
            layer + distance < depth, returned[distance - 1].astype(jnp.float32), 0.0
        )
    carried = carried.reshape(tok_rows, key_heads, 2 * head_dim)
    keys_back = rotate(carried[..., :head_dim], cosine_table, -sine_table)
    key_value_grad = (
        jnp.concatenate([keys_back, carried[..., head_dim:]], axis=-1)
        .astype(jnp.bfloat16)
        .reshape(tok_rows, -1)
    )
    query_grad_low = (
        rotate(query_grad.reshape(tok_rows, -1, head_dim), cosine_table, -sine_table)
        .astype(jnp.bfloat16)
        .reshape(tok_rows, -1)
    )
    query_grad_blocks, key_value_grad_blocks = exchange(
        sizes,
        "swap_projection",
        7,
        ("swap", query_grad_low.reshape(group, own, -1)),
        ("swap", key_value_grad.reshape(group, own, -1)),
    )
    grad_query = dot(normed_low, query_grad_low, 0, 0)
    grad_key_value = dot(normed_low, key_value_grad, 0, 0)
    grad_query = lax.psum(grad_query.astype(jnp.bfloat16), "dp").astype(jnp.float32)
    grad_key_value = lax.psum(grad_key_value.astype(jnp.bfloat16), "dp").astype(jnp.float32)

    attn_normed_grad = dot(wide(query_grad_blocks), query_full, 1, 1) + dot(
        wide(key_value_grad_blocks), key_value_full.reshape(width, -1), 1, 1
    )
    scale_own = lax.rsqrt(jnp.mean(tokens_own * tokens_own, axis=1, keepdims=True) + EPSILON)
    attn_dot = jnp.sum(attn_normed_grad * gains[0] * tokens_own, axis=1, keepdims=True)
    gain_attn_part = jnp.sum(attn_normed_grad * tokens_own * scale_own, axis=0)
    in_grad_own = (
        middle_grad
        + scale_own * gains[0] * attn_normed_grad
        - tokens_own * (scale_own**3 * attn_dot / width)
    ).astype(jnp.bfloat16)
    block_own = (middle + RESIDUAL_SCALE * moe_own.astype(jnp.float32)).astype(jnp.bfloat16)
    block_blocks, in_grad_blocks = exchange(
        sizes,
        "swap_results",
        8,
        ("swap", narrow(block_own)),
        ("swap", narrow(in_grad_own)),
    )
    gain_parts = jnp.stack([gain_attn_part, gain_moe_part]).astype(jnp.bfloat16)
    gain_sums = lax.psum(gain_parts, EVERY).astype(jnp.float32)
    gain_mine = lax.dynamic_slice_in_dim(gain_sums, me * feat_local, feat_local, 1)

    rows_late, grads_late, weights_late, block_blocks = lax.optimization_barrier(
        (rows_all, moe_grad_all, weights_all, block_blocks)
    )
    grad_expert_in, grad_expert_out = expert_grads(
        rows_late, grads_late, weights_late, in_flat, w_expert_out
    )
    rows_mine = lax.dynamic_slice_in_dim(rows_all, me * feat_local, feat_local, 1)
    grad_router = dot(rows_mine, logit_grad_all, 0, 0)
    return (
        block_blocks.reshape(tok_rows, feat_local),
        in_grad_blocks.reshape(tok_rows, feat_local),
        gain_mine[0],
        grad_query,
        grad_key_value.reshape(width, key_heads, -1),
        grad_output,
        gain_mine[1],
        grad_router,
        grad_expert_in,
        grad_expert_out,
    )


def solution(mesh):
    in_specs = (
        P("dp", ("row", "col")),
        P("dp", ("row", "col")),
        P("dp"),
        P("dp", None),
        P(("row", "col")),
        P(None, ("row", "col")),
        P(None, ("row", "col"), None),
        P(("row", "col"), None),
        P(("row", "col")),
        P(("row", "col"), None),
        P("row", None, None, "col"),
        P("row", "col", None),
    )
    out_specs = (
        P("dp", ("row", "col")),
        P("dp", ("row", "col")),
        P(("row", "col")),
        P(None, ("row", "col")),
        P(None, ("row", "col"), None),
        P(("row", "col"), None),
        P(("row", "col")),
        P(("row", "col"), None),
        P("row", None, None, "col"),
        P("row", "col", None),
    )
    sizes = (mesh.shape["row"], mesh.shape["col"], mesh.shape["dp"])
    return jax.shard_map(
        functools.partial(local, sizes),
        mesh=mesh,
        in_specs=in_specs,
        out_specs=out_specs,
        check_vma=False,
    )
```

time: 933 us -> 579 us (0.62)
  waiting for transfers between devices: 655 us -> 88.6 us
  Pallas kernels: 0 us -> 205 us
  blocking collectives: 82.4 us -> 156 us
  matrix products: 74.5 us -> 36.8 us
  starting transfers between devices: 20.9 us -> 0.32 us
    psum x2 -> x1, waiting for transfers between devices: 491 us -> 0.02 us  [local(): lax.psum(grad_query.astype(jnp.bfloat16), 'dp').astype(jnp.float32)]
    pallas_call x0 -> x11, Pallas kernels: none -> 205 us  [the longest x9 97.1 us: exchange(): pl.pallas_call(functools.partial(exchange_body, sizes, tuple(kinds)), out...]
    all_gather x1 -> x5, blocking collectives: 8.92 us -> 118 us  [gathered(): return lax.all_gather(array, axes, axis=axis, tiled=True)]
    unnamed x14 -> x8, waiting for transfers between devices: 90.8 us -> 2.64 us
    dot_general x29 -> x23, matrix products: 69.6 us -> 30.5 us  [the longest x9 16.5 us: dot(): lax.dot_general(a, b, (((left,), (right,)), ((), ())), preferred_element_...]
    unnamed x120 -> x123, local copies, waits for them, and re-layouts: 39.4 us -> 3.74 us
    all_gather x4 -> x6, waiting for transfers between devices: 58.3 us -> 85.9 us  [gathered(): return lax.all_gather(array, axes, axis=axis, tiled=True)]
    psum x4 -> x1, blocking collectives: 61.4 us -> 38.1 us  [local(): gain_sums = lax.psum(gain_parts, EVERY).astype(jnp.float32)]
  transfers between devices with their start and end apart: 16 -> 8, of which waited for: 14 -> 2; matrix products, arithmetic and copies ran while one was open for 7% -> 15% of each run, Pallas kernels for 0% -> 12%
where the time goes in v1:
time: 579 us; the launch traced here: 577 us
  Pallas kernels  205 us (35%)
  blocking collectives  156 us (27%)
  waiting for transfers between devices  88.6 us (15%)
  local copies, waits for them, and re-layouts  38.4 us (7%)
  other arithmetic  37.3 us (6%)
  matrix products  36.8 us (6%)
  between operations  15.2 us (3%)
    all_gather x5, blocking collectives, gathered(): return lax.all_gather(array, axes, axis=axis, tiled=True)  118 us
    pallas_call x9, Pallas kernels, exchange(): pl.pallas_call(functools.partial(exchange_body, sizes, tuple(kinds)), out...  97.1 us
    pallas_call x1, Pallas kernels, expert_grads(): pl.pallas_call(functools.partial(expert_grads_body, first_expert), grid=(...  88.1 us
    all_gather x6, waiting for transfers between devices, gathered(): return lax.all_gather(array, axes, axis=axis, tiled=True)  85.9 us
    psum x1, blocking collectives, local(): gain_sums = lax.psum(gain_parts, EVERY).astype(jnp.float32)  38.1 us
    pallas_call x1, Pallas kernels, local_experts(): pl.pallas_call(functools.partial(local_experts_body, first_expert), grid=...  19.6 us
    dot_general x9, matrix products, dot(): lax.dot_general(a, b, (((left,), (right,)), ((), ())), preferred_element_...  16.5 us
    reshape x1, local copies, waits for them, and re-layouts, local(): in_flat = w_expert_in.reshape(expert_local, width, 2 * hidden)  14 us
  transfers between devices with their start and end apart: 8, of which 2 were waited for; matrix products, arithmetic and copies ran while one was open for 15% of the time, Pallas kernels for 12%

profile of v1, /device:TPU:0, one launch (start us, length us, event | category | flops | bytes accessed | tf_op | source)
XLA Modules:
  0.0 577.4 jit_solution(1643377410458181396)
XLA Ops:
  8.7 10.3 %all_gather.33 = bf16[2,1024]{1,0:T(2,128)(2,1)S(1)} all-gather(bf16[2,128]{1,0:T(2,128)(2,1)S(1)} %pad_maximum_fusion.5), channel_id=1, replica_groups=mesh['dp'=4,'row'=4,'col'=2] {'row','col'}, dimensions={1}, use_global_device_ids=true | all-gather | bytes 4608 | tf_op jit(solution)/shard_map/all_gather | solution.py:359
  19.6 19.2 %gather_tokens.1 = (bf16[8,512,128]{2,1,0:T(8,128)(2,1)}, bf16[8,512,128]{2,1,0:T(8,128)(2,1)}) custom-call(bf16[512,128]{1,0:T(8,128)(2,1)} %refs_0_.1, bf16[512,128]{1,0:T(8,128)(2,1)} %refs_1_.1), custom_call_target="tpu_custom_call" | custom-call | tf_op jit(solution)/shard_map/gather_tokens/pallas_call | solution.py:129
  38.8 1.5 fusion
  40.8 1.6 fusion.2
  45.8 12.0 %all-gather = s32[4,1,512]{2,1,0:T(1,128)S(1)} all-gather(s32[1,1,512]{2,1,0:T(1,128)S(1)} %bitcast.410), channel_id=1, replica_groups=mesh['dp'=4,'row'=4,'col'=2] {'dp'}, dimensions={0}, use_global_device_ids=true | all-gather | bytes 10240 | tf_op jit(solution)/shard_map/all_gather | solution.py:359
  59.5 10.1 %shift_pairs.1 = bf16[2,512,128]{2,1,0:T(8,128)(2,1)} custom-call(bf16[512,128]{1,0:T(8,128)(2,1)} %maximum_bitcast_fusion.1.refs_0_), custom_call_target="tpu_custom_call" | custom-call | tf_op jit(solution)/shard_map/shift_pairs/pallas_call | solution.py:129
  69.7 1.6 slice_bitcast_fusion.6
  72.7 1.6 fusion.119
  79.3 5.6 swap_mixed.1
  85.0 14.0 %reshape.723.in_ref = bf16[8,1024,512]{2,1,0:T(8,128)(2,1)} reshape(bf16[8,1024,2,256]{3,2,1,0:T(2,128)(2,1)} %param.22) | data formatting | bytes 16777216 | tf_op jit(solution)/shard_map/reshape | solution.py:465
  99.0 9.1 %all_gather.38 = bf16[1024,32]{0,1:T(8,128)(2,1)S(1)} all-gather(bf16[128,32]{0,1:T(8,128)(2,1)S(1)} %copy-done.51), channel_id=1, replica_groups=mesh['dp'=4,'row'=4,'col'=2] {'row','col'}, dimensions={0}, use_global_device_ids=true | all-gather | bytes 73728 | tf_op jit(solution)/shard_map/all_gather | solution.py:359
  108.1 2.4 copy_bitcast_fusion.1
  112.9 2.2 multiply_reduce_fusion.2
  120.1 11.8 %gather_rows.1 = (bf16[8,64,1024]{2,1,0:T(8,128)(2,1)}, bf16[8,64,128]{2,1,0:T(8,128)(2,1)}) custom-call(bf16[64,1024]{1,0:T(8,128)(2,1)} %fusion.82.refs_0_, bf16[64,128]{1,0:T(8,128)(2,1)} %pad_maximum_fusion.3.refs_1_), custom_call_target="tpu_custom_call" | custom-call | tf_op jit(solution)/shard_map/gather_rows/pallas_call | solution.py:129
  133.0 1.8 maximum_add_fusion.weight_ref
  134.7 19.6 %local_experts.1 = (bf16[512,1024]{1,0:T(8,128)(2,1)}, bf16[512,1024]{1,0:T(8,128)(2,1)}, bf16[512,128]{1,0:T(8,128)(2,1)}) custom-call(bf16[512,1024]{1,0:T(8,128)(2,1)} %bitcast.382, bf16[512,1024]{1,0:T(8,128)(2,1)} %multiply_convert_fusion.1.grads_ref, f32[512,128]{1,0:T(8,128)} %maximum_add_fusion.weight_ref, bf16[8,1024,512]{2,1,0:T(8,128)(2,1)} %reshape.723.in_ref, ...), custom_call_target="tpu_custom_call" | custom-call | tf_op jit(solution)/shard_map/local_experts/pallas_call | solution.py:239
  154.3 16.7 %swap_back.1 = (bf16[8,64,1024]{2,1,0:T(8,128)(2,1)}, bf16[8,64,128]{2,1,0:T(8,128)(2,1)}) custom-call(bf16[8,64,1024]{2,1,0:T(8,128)(2,1)} %bitcast.383, bf16[8,64,128]{2,1,0:T(8,128)(2,1)} %bitcast.401), custom_call_target="tpu_custom_call" | custom-call | tf_op jit(solution)/shard_map/swap_back/pallas_call | solution.py:129
  171.0 2.1 convert_reduce_fusion
  174.7 1.6 copy.299
  177.3 1.9 multiply_reduce_fusion
  179.9 1.7 multiply_convert_fusion.3
  183.0 2.4 fusion.31
  186.1 5.5 swap_mixed_grad.1
  191.6 1.7 reshape.775
  194.5 1.6 fusion.94
  196.1 1.4 fusion.101
  197.5 1.5 fusion.6
  199.0 1.8 fusion.44
  213.6 12.7 %shift_grads.1 = bf16[2,512,128]{2,1,0:T(8,128)(2,1)} custom-call(bf16[2,512,128]{2,1,0:T(8,128)(2,1)} %pad_maximum_fusion.refs_0_), custom_call_target="tpu_custom_call" | custom-call | tf_op jit(solution)/shard_map/shift_grads/pallas_call | solution.py:129
  227.5 1.2 fusion.66
  228.8 1.4 fusion.19
  231.3 2.2 convolution_convert_fusion
  233.7 1.6 constant_dynamic-slice_fusion.2
  237.6 41.1 %all-gather.1 = bf16[32,64,32]{1,2,0:T(8,128)(2,1)S(1)} all-gather(bf16[1,64,32]{1,2,0:T(8,128)(2,1)S(1)} %copy.328), channel_id=1, replica_groups=mesh['dp'=4,'row'=4,'col'=2] {'dp','row','col'}, dimensions={0}, use_global_device_ids=true | all-gather | bytes 135168 | tf_op jit(solution)/shard_map/all_gather | solution.py:359
  280.7 6.8 %swap_projection.1 = (bf16[8,64,128]{2,1,0:T(8,128)(2,1)}, bf16[8,64,128]{2,1,0:T(8,128)(2,1)}) custom-call(bf16[8,64,128]{2,1,0:T(8,128)(2,1)} %copy.325.refs_0_, bf16[8,64,128]{2,1,0:T(8,128)(2,1)} %pad_maximum_fusion.2.refs_1_), custom_call_target="tpu_custom_call" | custom-call | tf_op jit(solution)/shard_map/swap_projection/pallas_call | solution.py:129
  287.6 2.4 convolution_bitcast_fusion
  290.1 2.5 fusion.78
  292.7 38.1 %psum.28 = bf16[2,1024]{1,0:T(2,128)(2,1)S(1)} all-reduce(bf16[2,1024]{1,0:T(2,128)(2,1)S(1)} %pad_maximum_fusion.4), channel_id=1, replica_groups=mesh['dp'=4,'row'=4,'col'=2] {'dp','row','col'}, use_global_device_ids=true, to_apply=%region_23.24 | all-reduce | flops 2048 | bytes 8192 | tf_op jit(solution)/shard_map/psum | solution.py:594
  331.3 45.4 %all_gather.39.weight_ref = bf16[2048,128]{1,0:T(8,128)(2,1)} all-gather(bf16[64,128]{1,0:T(8,128)(2,1)S(1)} %copy-done.37), channel_id=1, replica_groups=mesh['dp'=4,'row'=4,'col'=2] {'dp','row','col'}, dimensions={0}, use_global_device_ids=true | all-gather | bytes 540672 | tf_op jit(solution)/shard_map/all_gather | solution.py:359
  376.8 1.3 fusion.84
  379.4 8.7 %swap_results.1 = (bf16[8,64,128]{2,1,0:T(8,128)(2,1)}, bf16[8,64,128]{2,1,0:T(8,128)(2,1)}) custom-call(bf16[8,64,128]{2,1,0:T(8,128)(2,1)} %bitcast.387, bf16[8,64,128]{2,1,0:T(8,128)(2,1)} %bitcast.386), custom_call_target="tpu_custom_call" | custom-call | tf_op jit(solution)/shard_map/swap_results/pallas_call | solution.py:129
  388.1 1.8 convert_element_type.247
  389.9 1.8 reshape.744
  391.7 1.8 convert_element_type.252
  393.5 22.4 %all-gather.13.cloned.1.call-done.grads_ref = bf16[2048,1024]{1,0:T(8,128)(2,1)} async-done(((bf16[64,1024]{1,0:T(8,128)(2,1)}), bf16[2048,1024]{1,0:T(8,128)(2,1)}) %all-gather.13.cloned.1.call-update) | async-done | bytes 4194320 | tf_op jit(solution)/shard_map/all_gather | solution.py:359
  415.9 63.4 %all-gather.11.cloned.1.call-done.rows_ref = bf16[2048,1024]{1,0:T(8,128)(2,1)} async-done(((bf16[64,1024]{1,0:T(8,128)(2,1)}), bf16[2048,1024]{1,0:T(8,128)(2,1)}) %all-gather.11.cloned.1.call-update) | async-done | bytes 4194320 | tf_op jit(solution)/shard_map/all_gather | solution.py:359
  479.3 88.1 %expert_grads.1 = (f32[8,4096,128]{2,1,0:T(8,128)}, f32[8,256,1024]{2,1,0:T(8,128)}) custom-call(bf16[2048,1024]{1,0:T(8,128)(2,1)} %all-gather.11.cloned.1.call-done.rows_ref, bf16[2048,1024]{1,0:T(8,128)(2,1)} %all-gather.13.cloned.1.call-done.grads_ref, bf16[2048,128]{1,0:T(8,128)(2,1)} %all_gather.39.weight_ref, bf16[8,1024,512]{2,1,0:T(8,128)(2,1)} %reshape.723.in_ref, ...), custom_call_target="tpu_custom_call" | custom-call | tf_op jit(solution)/shard_map/expert_grads/pallas_call | solution.py:291
  567.4 1.9 fusion.54
  (227 shorter events, 51.3 us)
Async XLA Ops:
  7.2 50.6 %copy-start = (s32[512,8]{0,1:T(8,128)S(1)}, s32[512,8]{0,1:T(8,128)}, u32[]{:S(2)}) copy-start(s32[512,8]{0,1:T(8,128)} %param.15) | copy-start | bytes 49156
  7.2 105.7 %all-gather.9.cloned.1.call-start = ((), (), s32[]{:S(2)}) async-start(), calls=%async_computation.1 | async-start | bytes 2359296 | tf_op jit(solution)/shard_map/all_gather | solution.py:359
  7.9 223.4 %all-gather.19.cloned.1.call-start = ((), (), s32[]{:S(2)}) async-start(), calls=%async_computation.7 | async-start | bytes 1179648 | tf_op jit(solution)/shard_map/all_gather | solution.py:359
  8.0 36.5 %copy-start.54 = (f32[32]{0:T(128)}, f32[32]{0:T(128)S(1)}, u32[]{:S(2)}) copy-start(f32[32]{0:T(128)S(1)} %multiply_power_fusion) | copy-start | bytes 388
  19.0 25.6 %copy-start.43 = (f32[512]{0:T(512)}, f32[512]{0:T(512)S(1)}, u32[]{:S(2)}) copy-start(f32[512]{0:T(512)S(1)} %get-tuple-element.170) | copy-start | bytes 6148
  19.6 20.7 %copy-start.41 = (f32[1,1024]{1,0:T(1,128)}, f32[1,1024]{1,0:T(1,128)S(1)}, u32[]{:S(2)}) copy-start(f32[1,1024]{1,0:T(1,128)S(1)} %get-tuple-element.147) | copy-start | bytes 12292
  42.5 3.3 copy-start.47
  42.5 16.1 %copy-start.20 = (bf16[1024,128]{1,0:T(8,128)(2,1)S(1)}, bf16[1024,128]{1,0:T(8,128)(2,1)}, u32[]{:S(2)}) copy-start(bf16[1024,128]{1,0:T(8,128)(2,1)} %param.17) | copy-start | bytes 786436
  43.5 33.2 %copy-start.7 = (f32[512,1,128]{2,0,1:T(8,128)}, f32[512,1,128]{2,0,1:T(8,128)S(1)}, u32[]{:S(2)}) copy-start(f32[512,1,128]{2,0,1:T(8,128)S(1)} %convolution_bitcast_fusion.7) | copy-start | bytes 786436
  44.6 27.1 %copy-start.27 = (f32[512,32]{0,1:T(8,128)}, f32[512,32]{0,1:T(8,128)S(1)}, u32[]{:S(2)}) copy-start(f32[512,32]{0,1:T(8,128)S(1)} %get-tuple-element.153) | copy-start | bytes 196612
  45.8 26.0 %copy-start.13 = (bf16[512,1,32]{2,0,1:T(8,128)(2,1)}, bf16[512,1,32]{2,0,1:T(8,128)(2,1)S(1)}, u32[]{:S(2)}) copy-start(bf16[512,1,32]{2,0,1:T(8,128)(2,1)S(1)} %get-tuple-element.132) | copy-start | bytes 98308
  45.8 26.0 %copy-start.15 = (bf16[512,1,32]{2,0,1:T(8,128)(2,1)}, bf16[512,1,32]{2,0,1:T(8,128)(2,1)S(1)}, u32[]{:S(2)}) copy-start(bf16[512,1,32]{2,0,1:T(8,128)(2,1)S(1)} %get-tuple-element.133) | copy-start | bytes 98308
  71.3 5.9 %copy-start.11 = (bf16[512,1,128]{2,0,1:T(8,128)(2,1)}, bf16[512,1,128]{2,0,1:T(8,128)(2,1)S(1)}, u32[]{:S(2)}) copy-start(bf16[512,1,128]{2,0,1:T(8,128)(2,1)S(1)} %get-tuple-element.138) | copy-start | bytes 393220
  71.7 3.2 copy-start.22
  78.3 6.7 %copy-start.32 = (bf16[64,2,512]{2,0,1:T(8,128)(2,1)}, bf16[64,2,512]{2,0,1:T(8,128)(2,1)S(1)}, u32[]{:S(2)}) copy-start(bf16[64,2,512]{2,0,1:T(8,128)(2,1)S(1)} %fusion.28) | copy-start | bytes 393220
  85.0 14.0 %copy-start.51 = (bf16[128,32]{0,1:T(8,128)(2,1)S(1)}, bf16[128,32]{0,1:T(8,128)(2,1)}, u32[]{:S(2)}) copy-start(bf16[128,32]{0,1:T(8,128)(2,1)} %param.21) | copy-start | bytes 24580
  99.0 11.5 %copy-start.8 = (bf16[8,512,128]{2,1,0:T(8,128)(2,1)S(1)}, bf16[8,512,128]{2,1,0:T(8,128)(2,1)}, u32[]{:S(2)}) copy-start(bf16[8,512,128]{2,1,0:T(8,128)(2,1)} %get-tuple-element.30) | copy-start | bytes 3145732
  111.7 3.5 copy-start.36
  112.9 5.4 copy-start.34
  115.2 64.7 %copy-start.45 = (f32[64]{0:T(128)}, f32[64]{0:T(128)S(1)}, u32[]{:S(2)}) copy-start(f32[64]{0:T(128)S(1)} %add_rsqrt_fusion.2) | copy-start | bytes 772
  119.4 57.9 %copy-start.30 = (f32[64,32]{1,0:T(8,128)}, f32[64,32]{1,0:T(8,128)S(1)}, u32[]{:S(2)}) copy-start(f32[64,32]{1,0:T(8,128)S(1)} %get-tuple-element.125) | copy-start | bytes 24580
  177.1 8.3 %copy-start.28 = (f32[64,32]{1,0:T(8,128)}, f32[64,32]{1,0:T(8,128)S(1)}, u32[]{:S(2)}) copy-start(f32[64,32]{1,0:T(8,128)S(1)} %copy.301) | copy-start | bytes 24580
  177.3 8.1 %copy-start.52 = (f32[64]{0:T(128)}, f32[64]{0:T(128)S(1)}, u32[]{:S(2)}) copy-start(f32[64]{0:T(128)S(1)} %multiply_reduce_fusion.3) | copy-start | bytes 772
  179.8 11.8 %copy-start.56 = (f32[64]{0:T(128)}, f32[64]{0:T(128)S(1)}, u32[]{:S(2)}) copy-start(f32[64]{0:T(128)S(1)} %fusion.111) | copy-start | bytes 772
  181.6 106.0 %all-gather.17.cloned.1.call-start = ((), (), s32[]{:S(2)}) async-start(), calls=%async_computation.6 | async-start | bytes 2359296 | tf_op jit(solution)/shard_map/all_gather | solution.py:359
  182.3 107.7 %all-gather.15.cloned.1.call-start = ((), (), s32[]{:S(2)}) async-start(), calls=%async_computation.5 | async-start | bytes 2359296 | tf_op jit(solution)/shard_map/all_gather | solution.py:359
  182.9 193.9 %reduce-scatter.2.cloned.1.call-start = ((), (), s32[]{:S(2)}) async-start(), calls=%async_computation.4 | async-start | bytes 1179648 | tf_op jit(solution)/shard_map/reduce_scatter | solution.py:469
  209.3 16.9 %copy-start.19 = (f32[512,1,64]{2,0,1:T(8,128)S(1)}, f32[512,1,64]{2,0,1:T(8,128)}, u32[]{:S(2)}) copy-start(f32[512,1,64]{2,0,1:T(8,128)} %convolution_bitcast_fusion.5) | copy-start | bytes 393220
  209.3 16.9 %copy-start.21 = (f32[512,1,64]{2,0,1:T(8,128)S(1)}, f32[512,1,64]{2,0,1:T(8,128)}, u32[]{:S(2)}) copy-start(f32[512,1,64]{2,0,1:T(8,128)} %fusion.23) | copy-start | bytes 393220
  209.4 18.1 %copy-start.44 = (f32[512]{0:T(512)S(1)}, f32[512]{0:T(512)}, u32[]{:S(2)}) copy-start(f32[512]{0:T(512)} %copy-done.43) | copy-start | bytes 6148
  209.4 18.1 %copy-start.55 = (f32[32]{0:T(128)S(1)}, f32[32]{0:T(128)}, u32[]{:S(2)}) copy-start(f32[32]{0:T(128)} %copy-done.54) | copy-start | bytes 388
  209.4 178.7 %all-reduce.3.cloned.1.call-start = ((), (), s32[]{:S(2)}) async-start(), calls=%async_computation.8 | async-start | bytes 1572864 | tf_op jit(solution)/shard_map/psum | solution.py:571
  210.6 18.2 %copy-start.6 = (bf16[8,512,128]{2,1,0:T(8,128)(2,1)S(1)}, bf16[8,512,128]{2,1,0:T(8,128)(2,1)}, u32[]{:S(2)}) copy-start(bf16[8,512,128]{2,1,0:T(8,128)(2,1)} %get-tuple-element.29) | copy-start | bytes 3145732
  210.6 18.2 %copy-start.42 = (f32[1,1024]{1,0:T(1,128)S(1)}, f32[1,1024]{1,0:T(1,128)}, u32[]{:S(2)}) copy-start(f32[1,1024]{1,0:T(1,128)} %copy-done.41) | copy-start | bytes 12292
  210.6 18.2 %copy-start.50 = (f32[512]{0:T(512)S(1)}, f32[512]{0:T(512)}, u32[]{:S(2)}) copy-start(f32[512]{0:T(512)} %copy-done.49) | copy-start | bytes 6148
  231.3 6.1 %copy-start.29 = (f32[64,32]{1,0:T(8,128)S(1)}, f32[64,32]{1,0:T(8,128)}, u32[]{:S(2)}) copy-start(f32[64,32]{1,0:T(8,128)} %copy-done.28) | copy-start | bytes 24580
  231.3 6.1 %copy-start.31 = (f32[64,32]{1,0:T(8,128)S(1)}, f32[64,32]{1,0:T(8,128)}, u32[]{:S(2)}) copy-start(f32[64,32]{1,0:T(8,128)} %copy-done.30) | copy-start | bytes 24580
  231.3 6.1 %copy-start.53 = (f32[64]{0:T(128)S(1)}, f32[64]{0:T(128)}, u32[]{:S(2)}) copy-start(f32[64]{0:T(128)} %copy-done.52) | copy-start | bytes 772
  231.3 6.3 %copy-start.48 = (bf16[1024]{0:T(1024)(128)(2,1)S(1)}, bf16[1024]{0:T(1024)(128)(2,1)}, u32[]{:S(2)}) copy-start(bf16[1024]{0:T(1024)(128)(2,1)} %get-tuple-element.110) | copy-start | bytes 6148
  233.6 182.3 %all-gather.13.cloned.1.call-start = ((), (), s32[]{:S(2)}) async-start(), calls=%async_computation.3 | async-start | bytes 4325376 | tf_op jit(solution)/shard_map/all_gather | solution.py:359
  235.2 244.1 %all-gather.11.cloned.1.call-start = ((), (), s32[]{:S(2)}) async-start(), calls=%async_computation.2 | async-start | bytes 4325376 | tf_op jit(solution)/shard_map/all_gather | solution.py:359
  287.6 43.8 %copy-start.37 = (bf16[64,128]{1,0:T(8,128)(2,1)S(1)}, bf16[64,128]{1,0:T(8,128)(2,1)}, u32[]{:S(2)}) copy-start(bf16[64,128]{1,0:T(8,128)(2,1)} %pad_maximum_fusion.3.refs_1_) | copy-start | bytes 49156
  290.0 86.8 %copy-start.10 = (f32[64,1024]{1,0:T(8,128)S(1)}, f32[64,1024]{1,0:T(8,128)}, u32[]{:S(2)}) copy-start(f32[64,1024]{1,0:T(8,128)} %copy-done.9) | copy-start | bytes 786436
  290.0 86.7 %copy-start.46 = (f32[64]{0:T(128)S(1)}, f32[64]{0:T(128)}, u32[]{:S(2)}) copy-start(f32[64]{0:T(128)} %copy-done.45) | copy-start | bytes 772
  290.0 86.7 %copy-start.57 = (f32[64]{0:T(128)S(1)}, f32[64]{0:T(128)}, u32[]{:S(2)}) copy-start(f32[64]{0:T(128)} %copy-done.56) | copy-start | bytes 772
  479.3 89.9 %copy-start.40 = (bf16[8,64,128]{2,1,0:T(8,128)(2,1)S(1)}, bf16[8,64,128]{2,1,0:T(8,128)(2,1)}, u32[]{:S(2)}) copy-start(bf16[8,64,128]{2,1,0:T(8,128)(2,1)} %get-tuple-element.41) | copy-start | bytes 393220
  479.3 90.6 %copy-start.39 = (bf16[8,64,128]{2,1,0:T(8,128)(2,1)S(1)}, bf16[8,64,128]{2,1,0:T(8,128)(2,1)}, u32[]{:S(2)}) copy-start(bf16[8,64,128]{2,1,0:T(8,128)(2,1)} %get-tuple-element.42) | copy-start | bytes 393220
  479.3 91.2 %copy-start.1 = (s32[512,8]{0,1:T(8,128)S(1)}, s32[512,8]{0,1:T(8,128)}, u32[]{:S(2)}) copy-start(s32[512,8]{0,1:T(8,128)} %param.15) | copy-start | bytes 49156
  (19 other events, 36.2 us)
Sparse Core Ops, SparseCore 0:
  9.9 35.9 all-gather.8
  181.7 22.6 all-gather.18
  206.3 27.7 all-gather.16
  235.8 28.4 all-gather.14
  267.3 36.1 reduce-scatter.1
  306.5 45.1 all-reduce.2
  355.2 60.6 all-gather.12
  418.8 60.5 all-gather.10
